TPU v7x, 8 devices: a whole 2x2x1 slice. The times are simulated.
8 devices in a mesh: dp: 1 (over z), ep: 8 (over y, x, core).
Axes of the slice: x: 2, y: 2, z: 1, core: 2. Of those that a mesh axis runs over, the one named last changes fastest.
Arguments:
- x_in: bfloat16 [8, 16, 64, 1536], P(None, ('dp', 'ep'))
- dy_in: bfloat16 [8, 16, 64, 1536], P(None, ('dp', 'ep'))
- expert_id: int32 [8, 1, 16, 64, 8], P(None, None, ('dp', 'ep'))
- gate_vals: bfloat16 [8, 1, 16, 64, 8], P(None, None, ('dp', 'ep'))
- norm_attn: bfloat16 [1, 1536], replicated
- w_query: bfloat16 [1, 1536, 24, 64], replicated
- w_key: bfloat16 [1, 1536, 8, 64], replicated
- w_value: bfloat16 [1, 1536, 8, 64], replicated
- w_out: bfloat16 [1, 24, 64, 1536], replicated
- norm_ffn: bfloat16 [1, 1536], replicated
- s_gate: bfloat16 [1, 1536, 512], replicated
- s_up: bfloat16 [1, 1536, 512], replicated
- s_down: bfloat16 [1, 512, 1536], replicated
- e_gate: bfloat16 [1, 40, 1536, 512], P(None, 'ep')
- e_up: bfloat16 [1, 40, 1536, 512], P(None, 'ep')
- e_down: bfloat16 [1, 40, 512, 1536], P(None, 'ep')
Outputs:
- output 1: bfloat16 [8, 16, 64, 1536], P(None, ('dp', 'ep'))
- output 2: bfloat16 [8, 16, 64, 1536], P(None, ('dp', 'ep'))
- output 3: float32 [1, 1536], P('dp')
- output 4: float32 [1, 1536, 24, 64], P('dp')
- output 5: float32 [1, 1536, 8, 64], P('dp')
- output 6: float32 [1, 1536, 8, 64], P('dp')
- output 7: float32 [1, 24, 64, 1536], P('dp')
- output 8: float32 [1, 1536], P('dp')
- output 9: float32 [1, 1536, 512], P('dp')
- output 10: float32 [1, 1536, 512], P('dp')
- output 11: float32 [1, 512, 1536], P('dp')
- output 12: float32 [1, 40, 1536, 512], P('dp', 'ep')
- output 13: float32 [1, 40, 1536, 512], P('dp', 'ep')
- output 14: float32 [1, 40, 512, 1536], P('dp', 'ep')
All inputs are finite; a program needn't handle non-finite values.
Results may differ from a plain program's by a relative error of at most 0.02.
Values are sent between devices in bfloat16 or wider.
A program may use at most 1 GiB of HBM per device.

v0:
```python
import jax
import jax.numpy as jnp
from jax import lax
from jax.sharding import PartitionSpec as P

EPS = 1e-6
ROPE_BASE = 10000.0
CAP_FACTOR = 2


def capacity_of(tokens, top_k, n_exp):
    return 8 * ((CAP_FACTOR * tokens * top_k + 8 * n_exp - 1) // (8 * n_exp))


def rms_norm(values, gain_w):
    vals_f = values.astype(jnp.float32)
    inv_rms = lax.rsqrt(jnp.mean(vals_f * vals_f, axis=-1, keepdims=True) + EPS)
    return (vals_f * inv_rms * gain_w.astype(jnp.float32)).astype(jnp.bfloat16)


def rope_rotate(tensor, cos_t, sin_t):
    half_dim = tensor.shape[-1] // 2
    tens_f = tensor.astype(jnp.float32)
    first_half = tens_f[..., :half_dim]
    second_half = tens_f[..., half_dim:]
    return jnp.concatenate([first_half * cos_t - second_half * sin_t, second_half * cos_t + first_half * sin_t], axis=-1).astype(jnp.bfloat16)


def attn_block(act_in, norm_a, w_query, w_key, w_value, w_out, norm_f):
    n_seq = act_in.shape[0]
    seq_len = act_in.shape[1]
    kv_heads = w_key.shape[1]
    head_dim = w_key.shape[2]
    q_group = w_query.shape[1] // kv_heads
    normed = rms_norm(act_in, norm_a)
    query_heads = jnp.einsum('nsd,dhk->nshk', normed, w_query, preferred_element_type=jnp.float32).astype(jnp.bfloat16)
    key_heads = jnp.einsum('nsd,dhk->nshk', normed, w_key, preferred_element_type=jnp.float32).astype(jnp.bfloat16)
    value_heads = jnp.einsum('nsd,dhk->nshk', normed, w_value, preferred_element_type=jnp.float32).astype(jnp.bfloat16)
    position = jnp.arange(seq_len, dtype=jnp.float32)
    inv_freq = ROPE_BASE ** (-jnp.arange(head_dim // 2, dtype=jnp.float32) / (head_dim // 2))
    angle_t = position[:, None] * inv_freq[None, :]
    cos_t = jnp.cos(angle_t)[:, None, :]
    sin_t = jnp.sin(angle_t)[:, None, :]
    query_heads = rope_rotate(query_heads, cos_t, sin_t).reshape(n_seq, seq_len, kv_heads, q_group, head_dim)
    key_heads = rope_rotate(key_heads, cos_t, sin_t)
    scores = jnp.einsum('nqhgk,nshk->nhgqs', query_heads, key_heads, preferred_element_type=jnp.float32) * head_dim ** -0.5
    causal = jnp.arange(seq_len)[:, None] >= jnp.arange(seq_len)[None, :]
    attn_prob = jax.nn.softmax(jnp.where(causal, scores, -1e30), axis=-1).astype(jnp.bfloat16)
    mixed = jnp.einsum('nhgqs,nshk->nqhgk', attn_prob, value_heads, preferred_element_type=jnp.float32).astype(jnp.bfloat16)
    mixed = mixed.reshape(n_seq, seq_len, kv_heads * q_group, head_dim)
    attn_out = jnp.einsum('nqhk,hkd->nqd', mixed, w_out, preferred_element_type=jnp.float32)
    hidden = (act_in.astype(jnp.float32) + attn_out).astype(jnp.bfloat16)
    return hidden, rms_norm(hidden, norm_f)


def swiglu_shared(normed, s_gate, s_up, s_down):
    gate_act = jnp.einsum('nsd,df->nsf', normed, s_gate, preferred_element_type=jnp.float32).astype(jnp.bfloat16)
    up_act = jnp.einsum('nsd,df->nsf', normed, s_up, preferred_element_type=jnp.float32).astype(jnp.bfloat16)
    inner = (jax.nn.silu(gate_act.astype(jnp.float32)) * up_act.astype(jnp.float32)).astype(jnp.bfloat16)
    return jnp.einsum('nsf,fd->nsd', inner, s_down, preferred_element_type=jnp.float32)


def expert_forward(rows_in, e_gate, e_up, e_down):
    gate_act = jnp.einsum('nxcd,xdf->nxcf', rows_in, e_gate, preferred_element_type=jnp.float32).astype(jnp.bfloat16)
    up_act = jnp.einsum('nxcd,xdf->nxcf', rows_in, e_up, preferred_element_type=jnp.float32).astype(jnp.bfloat16)
    inner = (jax.nn.silu(gate_act.astype(jnp.float32)) * up_act.astype(jnp.float32)).astype(jnp.bfloat16)
    return jnp.einsum('nxcf,xfd->nxcd', inner, e_down, preferred_element_type=jnp.float32).astype(jnp.bfloat16)


def expert_backward(rows_in, d_out, e_gate, e_up, e_down):
    gate_f = jnp.einsum('nxcd,xdf->nxcf', rows_in, e_gate, preferred_element_type=jnp.float32).astype(jnp.bfloat16).astype(jnp.float32)
    up_f = jnp.einsum('nxcd,xdf->nxcf', rows_in, e_up, preferred_element_type=jnp.float32).astype(jnp.bfloat16).astype(jnp.float32)
    sig_gate = jax.nn.sigmoid(gate_f)
    silu_gate = gate_f * sig_gate
    inner = (silu_gate * up_f).astype(jnp.bfloat16)
    d_inner = jnp.einsum('nxcd,xfd->nxcf', d_out, e_down, preferred_element_type=jnp.float32).astype(jnp.bfloat16).astype(jnp.float32)
    d_gate = (d_inner * up_f * sig_gate * (1.0 + gate_f * (1.0 - sig_gate))).astype(jnp.bfloat16)
    d_up = (d_inner * silu_gate).astype(jnp.bfloat16)
    rows_from_gate = jnp.einsum('nxcf,xdf->nxcd', d_gate, e_gate, preferred_element_type=jnp.float32).astype(jnp.bfloat16)
    rows_from_up = jnp.einsum('nxcf,xdf->nxcd', d_up, e_up, preferred_element_type=jnp.float32).astype(jnp.bfloat16)
    d_rows = (rows_from_gate.astype(jnp.float32) + rows_from_up.astype(jnp.float32)).astype(jnp.bfloat16)
    g_gate = jnp.einsum('nxcd,nxcf->xdf', rows_in, d_gate, preferred_element_type=jnp.float32)
    g_up = jnp.einsum('nxcd,nxcf->xdf', rows_in, d_up, preferred_element_type=jnp.float32)
    g_down = jnp.einsum('nxcf,nxcd->xfd', inner, d_out, preferred_element_type=jnp.float32)
    return d_rows, g_gate, g_up, g_down


def place_rows(rows, position, n_rows):
    return jnp.zeros((n_rows, rows.shape[-1]), jnp.bfloat16).at[position].set(rows, unique_indices=True)


def expert_positions(choice_ids, n_exp, cap_rows):
    flat_ids = choice_ids.reshape(-1)
    one_hot = (flat_ids[:, None] == jnp.arange(n_exp)[None, :]).astype(jnp.int32)
    row_rank = jnp.sum((jnp.cumsum(one_hot, axis=0) - 1) * one_hot, axis=1)
    return (flat_ids * cap_rows + row_rank).reshape(choice_ids.shape)


def solution(mesh):
    n_ep = mesh.shape['ep']

    def device_fn(x_in, dy_in, expert_id, gate_vals, norm_attn, w_query, w_key, w_value, w_out, norm_ffn, s_gate, s_up, s_down, e_gate, e_up, e_down):
        n_slots, n_seq, seq_len, d_model = x_in.shape
        n_layers = w_query.shape[0]
        top_k = expert_id.shape[-1]
        local_e = e_gate.shape[1]
        n_exp = local_e * n_ep
        tokens = n_seq * seq_len
        cap_rows = capacity_of(tokens, top_k, n_exp)
        dense_all = (norm_attn, w_query, w_key, w_value, w_out, norm_ffn, s_gate, s_up, s_down)
        dense_acc = [[jnp.zeros(weight.shape[1:], jnp.float32) for weight in dense_all] for layer_idx in range(n_layers)]
        expert_acc = [[jnp.zeros(weight.shape[1:], jnp.float32) for weight in (e_gate, e_up, e_down)] for layer_idx in range(n_layers)]
        y_list = []
        dx_list = []
        for slot_idx in range(n_slots):
            act_in = x_in[slot_idx]
            saved_state = []
            for layer_idx in range(n_layers):
                choice_ids = expert_id[slot_idx, layer_idx].reshape(tokens, top_k)
                gate_row = gate_vals[slot_idx, layer_idx].reshape(tokens, top_k)
                position = expert_positions(choice_ids, n_exp, cap_rows)
                (hidden, normed), attn_pull = jax.vjp(attn_block, act_in, norm_attn[layer_idx], w_query[layer_idx], w_key[layer_idx], w_value[layer_idx], w_out[layer_idx], norm_ffn[layer_idx])
                shared_out, shared_pull = jax.vjp(swiglu_shared, normed, s_gate[layer_idx], s_up[layer_idx], s_down[layer_idx])
                send_rows = place_rows(normed.reshape(tokens, 1, d_model), position, n_exp * cap_rows).reshape(n_ep, local_e, cap_rows, d_model)
                recv_rows = lax.all_to_all(send_rows, 'ep', 0, 0, tiled=True)
                expert_res = expert_forward(recv_rows, e_gate[layer_idx], e_up[layer_idx], e_down[layer_idx])
                returned = lax.all_to_all(expert_res, 'ep', 0, 0, tiled=True).reshape(n_exp * cap_rows, d_model)
                routed = jnp.einsum('tk,tkd->td', gate_row, returned[position], preferred_element_type=jnp.float32)
                act_in = (hidden.astype(jnp.float32) + shared_out + routed.reshape(n_seq, seq_len, d_model)).astype(jnp.bfloat16)
                saved_state.append((attn_pull, shared_pull, recv_rows, position, gate_row))
            y_list.append(act_in)
            grad_act = dy_in[slot_idx]
            for layer_idx in reversed(range(n_layers)):
                attn_pull, shared_pull, recv_rows, position, gate_row = saved_state[layer_idx]
                scaled = (gate_row.astype(jnp.float32)[:, :, None] * grad_act.reshape(tokens, 1, d_model).astype(jnp.float32)).astype(jnp.bfloat16)
                send_grad = place_rows(scaled, position, n_exp * cap_rows).reshape(n_ep, local_e, cap_rows, d_model)
                recv_grad = lax.all_to_all(send_grad, 'ep', 0, 0, tiled=True)
                d_rows, g_gate, g_up, g_down = expert_backward(recv_rows, recv_grad, e_gate[layer_idx], e_up[layer_idx], e_down[layer_idx])
                d_returned = lax.all_to_all(d_rows, 'ep', 0, 0, tiled=True).reshape(n_exp * cap_rows, d_model)
                d_routed = jnp.sum(d_returned[position], axis=1, dtype=jnp.float32).astype(jnp.bfloat16)
                shared_cts = shared_pull(grad_act.astype(jnp.float32))
                d_normed = (d_routed.reshape(n_seq, seq_len, d_model).astype(jnp.float32) + shared_cts[0].astype(jnp.float32)).astype(jnp.bfloat16)
                attn_cts = attn_pull((grad_act, d_normed))
                grad_act = attn_cts[0]
                new_dense = list(attn_cts[1:]) + list(shared_cts[1:])
                dense_acc[layer_idx] = [acc_g + new_g.astype(jnp.float32) for acc_g, new_g in zip(dense_acc[layer_idx], new_dense)]
                expert_acc[layer_idx] = [acc_g + new_g.astype(jnp.bfloat16).astype(jnp.float32) for acc_g, new_g in zip(expert_acc[layer_idx], (g_gate, g_up, g_down))]
            dx_list.append(grad_act)
        dense_out = [jnp.stack([dense_acc[layer_idx][w_idx] for layer_idx in range(n_layers)]) for w_idx in range(9)]
        dense_out = lax.psum(dense_out, 'ep')
        expert_out = [jnp.stack([expert_acc[layer_idx][w_idx] for layer_idx in range(n_layers)]) for w_idx in range(3)]
        return tuple([jnp.stack(y_list), jnp.stack(dx_list)] + list(dense_out) + expert_out)

    tok_spec = P(None, ('dp', 'ep'), None, None)
    route_spec = P(None, None, ('dp', 'ep'), None, None)
    rep_spec = P()
    exp_spec = P(None, 'ep', None, None)
    vec_grad = P('dp', None)
    mat_grad = P('dp', None, None)
    head_grad = P('dp', None, None, None)
    exp_grad = P('dp', 'ep', None, None)
    in_specs = (tok_spec, tok_spec, route_spec, route_spec) + (rep_spec,) * 9 + (exp_spec,) * 3
    out_specs = (tok_spec, tok_spec, vec_grad, head_grad, head_grad, head_grad, head_grad, vec_grad, mat_grad, mat_grad, mat_grad, exp_grad, exp_grad, exp_grad)
    return jax.shard_map(device_fn, mesh=mesh, in_specs=in_specs, out_specs=out_specs, check_vma=False)
```

profile of v0, /device:TPU:0, one launch (start us, length us, event | category | flops | bytes accessed | tf_op | source)
XLA Modules:
  0.0 3242.1 jit_solution(14312105434808521433)
XLA Ops:
  90.8 63.4 %all-to-all-done.12 = bf16[8,5,56,1536]{3,2,1,0:T(8,128)(2,1)} async-done(((bf16[8,5,56,1536]{3,2,1,0:T(8,128)(2,1)}), bf16[8,5,56,1536]{3,2,1,0:T(8,128)(2,1)}, u32[]{:S(2)}, u32[]{:S(2)}) %all-to-all-start.12) | async-done | bytes 6881312 | tf_op jit(solution)/shard_map/all_to_all | solution.py:125
  180.5 55.3 %all-to-all-done.28 = bf16[8,5,56,1536]{3,2,1,0:T(8,128)(2,1)} async-done(((bf16[8,5,56,1536]{3,2,1,0:T(8,128)(2,1)}), bf16[8,5,56,1536]{3,2,1,0:T(8,128)(2,1)}, u32[]{:S(2)}, u32[]{:S(2)}) %all-to-all-start.28) | async-done | bytes 6881312 | tf_op jit(solution)/shard_map/all_to_all | solution.py:137
  260.2 14.1 fusion.245
  284.9 12.9 fusion.102
  304.2 12.9 all-to-all-done.26
  383.9 14.7 all-to-all-done.29
  460.9 19.1 all-to-all-done.24
  531.1 30.6 all-to-all-done.10
  586.0 14.2 fusion.249
  610.9 12.7 fusion.101
  630.1 13.0 all-to-all-done.22
  756.0 11.5 gather_fusion.13
  804.5 21.0 all-to-all-done.30
  871.4 35.5 %all-to-all-done.8 = bf16[8,5,56,1536]{3,2,1,0:T(8,128)(2,1)} async-done(((bf16[8,5,56,1536]{3,2,1,0:T(8,128)(2,1)}), bf16[8,5,56,1536]{3,2,1,0:T(8,128)(2,1)}, u32[]{:S(2)}, u32[]{:S(2)}) %all-to-all-start.8) | async-done | bytes 6881312 | tf_op jit(solution)/shard_map/all_to_all | solution.py:125
  931.2 14.2 fusion.253
  956.0 12.7 fusion.100
  975.1 13.3 all-to-all-done.13
  1002.9 12.0 fusion.106
  1054.2 15.5 all-to-all-done.25
  1131.8 19.7 all-to-all-done.11
  1166.4 12.0 fusion.109
  1178.3 11.5 gather_fusion.5
  1218.8 14.3 all-to-all-done.6
  1257.5 14.0 fusion.257
  1282.1 13.1 fusion.99
  1301.6 12.9 all-to-all-done.14
  1338.7 14.1 fusion.241
  1363.4 12.7 fusion.103
  1382.5 13.3 all-to-all-done.23
  1416.0 12.1 fusion.112
  1433.5 43.8 %all-to-all-done.31 = bf16[8,5,56,1536]{3,2,1,0:T(8,128)(2,1)} async-done(((bf16[8,5,56,1536]{3,2,1,0:T(8,128)(2,1)}), bf16[8,5,56,1536]{3,2,1,0:T(8,128)(2,1)}, u32[]{:S(2)}, u32[]{:S(2)}) %all-to-all-start.31) | async-done | bytes 6881312 | tf_op jit(solution)/shard_map/all_to_all | solution.py:139
  1506.5 11.5 gather_fusion.15
  1587.8 52.8 %all-to-all-done.9 = bf16[8,5,56,1536]{3,2,1,0:T(8,128)(2,1)} async-done(((bf16[8,5,56,1536]{3,2,1,0:T(8,128)(2,1)}), bf16[8,5,56,1536]{3,2,1,0:T(8,128)(2,1)}, u32[]{:S(2)}, u32[]{:S(2)}) %all-to-all-start.9) | async-done | bytes 6881312 | tf_op jit(solution)/shard_map/all_to_all | solution.py:127
  1700.8 21.2 all-to-all-done.7
  1747.7 11.5 gather_fusion.4
  1791.2 12.1 all-to-all-done
  1827.7 14.2 fusion.269
  1852.5 12.7 fusion.96
  1871.6 13.1 all-to-all-done.15
  1899.4 12.0 fusion.115
  1922.7 11.6 gather_fusion.7
  2006.3 11.5 gather_fusion.8
  2035.1 12.7 all-to-all-done.1
  2097.1 32.2 all-to-all-done.4
  2133.3 12.0 fusion.124
  2184.4 26.8 all-to-all-done.20
  2211.1 14.1 fusion.261
  2235.8 12.6 fusion.98
  2286.7 12.4 fusion.118
  2299.1 37.2 %all-to-all-done.21 = bf16[8,5,56,1536]{3,2,1,0:T(8,128)(2,1)} async-done(((bf16[8,5,56,1536]{3,2,1,0:T(8,128)(2,1)}), bf16[8,5,56,1536]{3,2,1,0:T(8,128)(2,1)}, u32[]{:S(2)}, u32[]{:S(2)}) %all-to-all-start.21) | async-done | bytes 6881312 | tf_op jit(solution)/shard_map/all_to_all | solution.py:139
  2421.2 11.5 gather_fusion.2
  2465.8 33.3 %all-to-all-done.2 = bf16[8,5,56,1536]{3,2,1,0:T(8,128)(2,1)} async-done(((bf16[8,5,56,1536]{3,2,1,0:T(8,128)(2,1)}), bf16[8,5,56,1536]{3,2,1,0:T(8,128)(2,1)}, u32[]{:S(2)}, u32[]{:S(2)}) %all-to-all-start.2) | async-done | bytes 6881312 | tf_op jit(solution)/shard_map/all_to_all | solution.py:125
  2546.1 34.6 %all-to-all-done.18 = bf16[8,5,56,1536]{3,2,1,0:T(8,128)(2,1)} async-done(((bf16[8,5,56,1536]{3,2,1,0:T(8,128)(2,1)}), bf16[8,5,56,1536]{3,2,1,0:T(8,128)(2,1)}, u32[]{:S(2)}, u32[]{:S(2)}) %all-to-all-start.18) | async-done | bytes 6881312 | tf_op jit(solution)/shard_map/all_to_all | solution.py:137
  2580.7 14.2 fusion.265
  2605.6 12.5 fusion.97
  2646.0 11.9 fusion.121
  2657.9 28.8 add_bitcast_fusion.1
  2686.8 19.5 all-to-all-done.19
  2767.2 12.5 add_bitcast_fusion.3
  2793.2 14.7 add_bitcast_fusion.4
  2819.0 29.0 add_bitcast_fusion
  2848.1 29.2 add_bitcast_fusion.2
  2913.5 24.8 all-reduce.32
  2957.8 251.2 %all-reduce.36.cloned.1.call-done = (f32[1,1536,24,64]{1,3,2,0:T(8,128)}, f32[1,1536,8,64]{1,3,2,0:T(8,128)}, f32[1,1536,8,64]{1,3,2,0:T(8,128)}, f32[1,24,64,15...) async-done(((f32[1,1536,24,64]{1,3,2,0:T(8,128)}, f32[1,1536,8,64]{1,3,2,0:T(8,128)}, f32[1,1536,8,64]{1,3,2,0:T(8,128)}, ...) | async-done | bytes 34603024 | tf_op jit(solution)/shard_map/psum | solution.py:150
  (2195 shorter events, 1754.9 us)
Async XLA Ops:
  7.2 402.0 %copy-start = (bf16[1,512,1536]{2,1,0:T(8,128)(2,1)S(1)}, bf16[1,512,1536]{2,1,0:T(8,128)(2,1)}, u32[]{:S(2)}) copy-start(bf16[1,512,1536]{2,1,0:T(8,128)(2,1)} %param.28) | copy-start | bytes 4718596
  8.0 35.9 %copy-start.323 = (f32[1536]{0:T(1024)}, f32[1536]{0:T(1024)S(1)}, u32[]{:S(2)}) copy-start(f32[1536]{0:T(1024)S(1)} %convert_reduce_fusion.1) | copy-start | bytes 18436
  11.5 32.5 %copy-start.641 = (f32[2,64]{1,0:T(2,128)}, f32[2,64]{1,0:T(2,128)S(1)}, u32[]{:S(2)}) copy-start(f32[2,64]{1,0:T(2,128)S(1)} %fusion.1731) | copy-start | bytes 1540
  49.7 744.0 %copy-start.267 = (f32[1536]{0:T(1024)}, f32[1536]{0:T(1024)S(1)}, u32[]{:S(2)}) copy-start(f32[1536]{0:T(1024)S(1)} %convert_reduce_fusion) | copy-start | bytes 18436
  71.7 82.6 %all-to-all-start.12 = ((bf16[8,5,56,1536]{3,2,1,0:T(8,128)(2,1)}), bf16[8,5,56,1536]{3,2,1,0:T(8,128)(2,1)}, u32[]{:S(2)}, u32[]{:S(2)}) async-start(bf16[8,5,56,1536]{3,2,1,0:T(8,128)(2,1)} %bitcast.3699), calls=%async_computation.12 | async-start | bytes 13762560 | tf_op jit(solution)/shard_map/all_to_all | solution.py:125
  154.3 81.5 %all-to-all-start.28 = ((bf16[8,5,56,1536]{3,2,1,0:T(8,128)(2,1)}), bf16[8,5,56,1536]{3,2,1,0:T(8,128)(2,1)}, u32[]{:S(2)}, u32[]{:S(2)}) async-start(bf16[8,5,56,1536]{3,2,1,0:T(8,128)(2,1)} %bitcast.3707), calls=%async_computation.28 | async-start | bytes 13762560 | tf_op jit(solution)/shard_map/all_to_all | solution.py:137
  235.8 81.4 %all-to-all-start.26 = ((bf16[8,5,56,1536]{3,2,1,0:T(8,128)(2,1)}), bf16[8,5,56,1536]{3,2,1,0:T(8,128)(2,1)}, u32[]{:S(2)}, u32[]{:S(2)}) async-start(bf16[8,5,56,1536]{3,2,1,0:T(8,128)(2,1)} %bitcast.3708), calls=%async_computation.26 | async-start | bytes 13762560 | tf_op jit(solution)/shard_map/all_to_all | solution.py:137
  317.1 81.4 %all-to-all-start.29 = ((bf16[8,5,56,1536]{3,2,1,0:T(8,128)(2,1)}), bf16[8,5,56,1536]{3,2,1,0:T(8,128)(2,1)}, u32[]{:S(2)}, u32[]{:S(2)}) async-start(bf16[8,5,56,1536]{3,2,1,0:T(8,128)(2,1)} %copy.582), calls=%async_computation.29 | async-start | bytes 13762560 | tf_op jit(solution)/shard_map/all_to_all | solution.py:139
  343.8 58.5 %copy-start.217 = (bf16[2,64,8,3,32]{4,1,3,2,0:T(8,128)(2,1)}, bf16[2,64,8,3,32]{4,1,3,2,0:T(8,128)(2,1)S(1)}, u32[]{:S(2)}) copy-start(bf16[2,64,8,3,32]{4,1,3,2,0:T(8,128)(2,1)S(1)} %copy.390) | copy-start | bytes 589828
  383.9 29.5 copy-start.163
  398.5 81.5 %all-to-all-start.24 = ((bf16[8,5,56,1536]{3,2,1,0:T(8,128)(2,1)}), bf16[8,5,56,1536]{3,2,1,0:T(8,128)(2,1)}, u32[]{:S(2)}, u32[]{:S(2)}) async-start(bf16[8,5,56,1536]{3,2,1,0:T(8,128)(2,1)} %bitcast.3706), calls=%async_computation.24 | async-start | bytes 13762560 | tf_op jit(solution)/shard_map/all_to_all | solution.py:137
  480.1 81.5 %all-to-all-start.10 = ((bf16[8,5,56,1536]{3,2,1,0:T(8,128)(2,1)}), bf16[8,5,56,1536]{3,2,1,0:T(8,128)(2,1)}, u32[]{:S(2)}, u32[]{:S(2)}) async-start(bf16[8,5,56,1536]{3,2,1,0:T(8,128)(2,1)} %bitcast.3694), calls=%async_computation.10 | async-start | bytes 13762560 | tf_op jit(solution)/shard_map/all_to_all | solution.py:125
  483.8 37.4 %copy-start.531 = (s32[1,1,2,64,8]{3,4,2,1,0:T(8,128)S(1)}, s32[1,1,2,64,8]{3,4,2,1,0:T(8,128)}, u32[]{:S(2)}) copy-start(s32[1,1,2,64,8]{3,4,2,1,0:T(8,128)} %get-tuple-element.219) | copy-start | bytes 12292
  483.8 37.5 %copy-start.313 = (bf16[1,2,64,1536]{3,2,1,0:T(8,128)(2,1)S(1)}, bf16[1,2,64,1536]{3,2,1,0:T(8,128)(2,1)}, u32[]{:S(2)}) copy-start(bf16[1,2,64,1536]{3,2,1,0:T(8,128)(2,1)} %get-tuple-element.118) | copy-start | bytes 1179652
  561.7 81.4 %all-to-all-start.22 = ((bf16[8,5,56,1536]{3,2,1,0:T(8,128)(2,1)}), bf16[8,5,56,1536]{3,2,1,0:T(8,128)(2,1)}, u32[]{:S(2)}, u32[]{:S(2)}) async-start(bf16[8,5,56,1536]{3,2,1,0:T(8,128)(2,1)} %bitcast.3709), calls=%async_computation.22 | async-start | bytes 13762560 | tf_op jit(solution)/shard_map/all_to_all | solution.py:137
  630.0 29.4 copy-start.555
  630.0 29.6 copy-start.530
  630.0 30.5 copy-start.630
  630.1 31.2 copy-start.570
  643.0 100.9 %all-to-all-start.27 = ((bf16[8,5,56,1536]{3,2,1,0:T(8,128)(2,1)}), bf16[8,5,56,1536]{3,2,1,0:T(8,128)(2,1)}, u32[]{:S(2)}, u32[]{:S(2)}) async-start(bf16[8,5,56,1536]{3,2,1,0:T(8,128)(2,1)} %copy.573), calls=%async_computation.27 | async-start | bytes 13762560 | tf_op jit(solution)/shard_map/all_to_all | solution.py:139
  646.6 40.0 %copy-start.553 = (s32[1024]{0:T(1024)S(1)}, s32[1024]{0:T(1024)}, u32[]{:S(2)}) copy-start(s32[1024]{0:T(1024)} %eq.208) | copy-start | bytes 12292
  646.7 40.2 %copy-start.528 = (s32[1,1,2,64,8]{3,4,2,1,0:T(8,128)S(1)}, s32[1,1,2,64,8]{3,4,2,1,0:T(8,128)}, u32[]{:S(2)}) copy-start(s32[1,1,2,64,8]{3,4,2,1,0:T(8,128)} %get-tuple-element.213) | copy-start | bytes 12292
  646.7 40.5 %copy-start.622 = (bf16[128,8]{0,1:T(8,128)(2,1)S(1)}, bf16[128,8]{0,1:T(8,128)(2,1)}, u32[]{:S(2)}) copy-start(bf16[128,8]{0,1:T(8,128)(2,1)} %reshape_squeeze.33) | copy-start | bytes 6148
  646.7 41.3 %copy-start.620 = (bf16[128,8,1]{0,1,2:T(8,128)(2,1)S(1)}, bf16[128,8,1]{0,1,2:T(8,128)(2,1)}, u32[]{:S(2)}) copy-start(bf16[128,8,1]{0,1,2:T(8,128)(2,1)} %reshape.2016) | copy-start | bytes 6148
  646.7 42.0 %copy-start.621 = (bf16[128,8,1]{0,1,2:T(8,128)(2,1)S(1)}, bf16[128,8,1]{0,1,2:T(8,128)(2,1)}, u32[]{:S(2)}) copy-start(bf16[128,8,1]{0,1,2:T(8,128)(2,1)} %reshape.2010) | copy-start | bytes 6148
  646.7 42.7 %copy-start.623 = (bf16[128,8,1]{0,1,2:T(8,128)(2,1)S(1)}, bf16[128,8,1]{0,1,2:T(8,128)(2,1)}, u32[]{:S(2)}) copy-start(bf16[128,8,1]{0,1,2:T(8,128)(2,1)} %reshape.2004) | copy-start | bytes 6148
  646.7 43.5 %copy-start.624 = (bf16[128,8,1]{0,1,2:T(8,128)(2,1)S(1)}, bf16[128,8,1]{0,1,2:T(8,128)(2,1)}, u32[]{:S(2)}) copy-start(bf16[128,8,1]{0,1,2:T(8,128)(2,1)} %reshape.2022) | copy-start | bytes 6148
  646.8 44.1 %copy-start.625 = (bf16[128,8,1]{0,1,2:T(8,128)(2,1)S(1)}, bf16[128,8,1]{0,1,2:T(8,128)(2,1)}, u32[]{:S(2)}) copy-start(bf16[128,8,1]{0,1,2:T(8,128)(2,1)} %reshape.2028) | copy-start | bytes 6148
  646.8 44.8 %copy-start.626 = (bf16[128,8,1]{0,1,2:T(8,128)(2,1)S(1)}, bf16[128,8,1]{0,1,2:T(8,128)(2,1)}, u32[]{:S(2)}) copy-start(bf16[128,8,1]{0,1,2:T(8,128)(2,1)} %reshape.2034) | copy-start | bytes 6148
  647.5 44.9 %copy-start.627 = (bf16[128,8,1]{0,1,2:T(8,128)(2,1)S(1)}, bf16[128,8,1]{0,1,2:T(8,128)(2,1)}, u32[]{:S(2)}) copy-start(bf16[128,8,1]{0,1,2:T(8,128)(2,1)} %reshape.2040) | copy-start | bytes 6148
  647.6 45.5 %copy-start.628 = (bf16[128,8,1]{0,1,2:T(8,128)(2,1)S(1)}, bf16[128,8,1]{0,1,2:T(8,128)(2,1)}, u32[]{:S(2)}) copy-start(bf16[128,8,1]{0,1,2:T(8,128)(2,1)} %reshape.2046) | copy-start | bytes 6148
  647.7 46.3 %copy-start.312 = (bf16[1,2,64,1536]{3,2,1,0:T(8,128)(2,1)S(1)}, bf16[1,2,64,1536]{3,2,1,0:T(8,128)(2,1)}, u32[]{:S(2)}) copy-start(bf16[1,2,64,1536]{3,2,1,0:T(8,128)(2,1)} %get-tuple-element.121) | copy-start | bytes 1179652
  687.2 142.2 %copy-start.557 = (s32[1024]{0:T(1024)}, s32[1024]{0:T(1024)S(1)}, u32[]{:S(2)}) copy-start(s32[1024]{0:T(1024)S(1)} %reshape.1836) | copy-start | bytes 12292
  743.9 81.5 %all-to-all-start.30 = ((bf16[8,5,56,1536]{3,2,1,0:T(8,128)(2,1)}), bf16[8,5,56,1536]{3,2,1,0:T(8,128)(2,1)}, u32[]{:S(2)}, u32[]{:S(2)}) async-start(bf16[8,5,56,1536]{3,2,1,0:T(8,128)(2,1)} %bitcast.3705), calls=%async_computation.30 | async-start | bytes 13762560 | tf_op jit(solution)/shard_map/all_to_all | solution.py:137
  825.4 81.6 %all-to-all-start.8 = ((bf16[8,5,56,1536]{3,2,1,0:T(8,128)(2,1)}), bf16[8,5,56,1536]{3,2,1,0:T(8,128)(2,1)}, u32[]{:S(2)}, u32[]{:S(2)}) async-start(bf16[8,5,56,1536]{3,2,1,0:T(8,128)(2,1)} %bitcast.3700), calls=%async_computation.8 | async-start | bytes 13762560 | tf_op jit(solution)/shard_map/all_to_all | solution.py:125
  907.0 81.4 %all-to-all-start.13 = ((bf16[8,5,56,1536]{3,2,1,0:T(8,128)(2,1)}), bf16[8,5,56,1536]{3,2,1,0:T(8,128)(2,1)}, u32[]{:S(2)}, u32[]{:S(2)}) async-start(bf16[8,5,56,1536]{3,2,1,0:T(8,128)(2,1)} %copy.507), calls=%async_computation.13 | async-start | bytes 13762560 | tf_op jit(solution)/shard_map/all_to_all | solution.py:127
  988.4 81.4 %all-to-all-start.25 = ((bf16[8,5,56,1536]{3,2,1,0:T(8,128)(2,1)}), bf16[8,5,56,1536]{3,2,1,0:T(8,128)(2,1)}, u32[]{:S(2)}, u32[]{:S(2)}) async-start(bf16[8,5,56,1536]{3,2,1,0:T(8,128)(2,1)} %copy.564), calls=%async_computation.25 | async-start | bytes 13762560 | tf_op jit(solution)/shard_map/all_to_all | solution.py:139
  1069.7 81.8 %all-to-all-start.11 = ((bf16[8,5,56,1536]{3,2,1,0:T(8,128)(2,1)}), bf16[8,5,56,1536]{3,2,1,0:T(8,128)(2,1)}, u32[]{:S(2)}, u32[]{:S(2)}) async-start(bf16[8,5,56,1536]{3,2,1,0:T(8,128)(2,1)} %copy.490), calls=%async_computation.11 | async-start | bytes 13762560 | tf_op jit(solution)/shard_map/all_to_all | solution.py:127
  1151.5 81.6 %all-to-all-start.6 = ((bf16[8,5,56,1536]{3,2,1,0:T(8,128)(2,1)}), bf16[8,5,56,1536]{3,2,1,0:T(8,128)(2,1)}, u32[]{:S(2)}, u32[]{:S(2)}) async-start(bf16[8,5,56,1536]{3,2,1,0:T(8,128)(2,1)} %bitcast.3696), calls=%async_computation.6 | async-start | bytes 13762560 | tf_op jit(solution)/shard_map/all_to_all | solution.py:125
  1233.1 81.4 %all-to-all-start.14 = ((bf16[8,5,56,1536]{3,2,1,0:T(8,128)(2,1)}), bf16[8,5,56,1536]{3,2,1,0:T(8,128)(2,1)}, u32[]{:S(2)}, u32[]{:S(2)}) async-start(bf16[8,5,56,1536]{3,2,1,0:T(8,128)(2,1)} %bitcast.3701), calls=%async_computation.14 | async-start | bytes 13762560 | tf_op jit(solution)/shard_map/all_to_all | solution.py:125
  1314.5 81.4 %all-to-all-start.23 = ((bf16[8,5,56,1536]{3,2,1,0:T(8,128)(2,1)}), bf16[8,5,56,1536]{3,2,1,0:T(8,128)(2,1)}, u32[]{:S(2)}, u32[]{:S(2)}) async-start(bf16[8,5,56,1536]{3,2,1,0:T(8,128)(2,1)} %copy.555), calls=%async_computation.23 | async-start | bytes 13762560 | tf_op jit(solution)/shard_map/all_to_all | solution.py:139
  1395.8 81.4 %all-to-all-start.31 = ((bf16[8,5,56,1536]{3,2,1,0:T(8,128)(2,1)}), bf16[8,5,56,1536]{3,2,1,0:T(8,128)(2,1)}, u32[]{:S(2)}, u32[]{:S(2)}) async-start(bf16[8,5,56,1536]{3,2,1,0:T(8,128)(2,1)} %copy.591), calls=%async_computation.31 | async-start | bytes 13762560 | tf_op jit(solution)/shard_map/all_to_all | solution.py:139
  1477.3 81.7 %all-to-all-start.16 = ((bf16[8,5,56,1536]{3,2,1,0:T(8,128)(2,1)}), bf16[8,5,56,1536]{3,2,1,0:T(8,128)(2,1)}, u32[]{:S(2)}, u32[]{:S(2)}) async-start(bf16[8,5,56,1536]{3,2,1,0:T(8,128)(2,1)} %bitcast.3704), calls=%async_computation.16 | async-start | bytes 13762560 | tf_op jit(solution)/shard_map/all_to_all | solution.py:137
  1530.7 136.7 %copy-start.169 = (bf16[2,64,1536]{2,1,0:T(8,128)(2,1)}, bf16[2,64,1536]{2,1,0:T(8,128)(2,1)S(1)}, u32[]{:S(2)}) copy-start(bf16[2,64,1536]{2,1,0:T(8,128)(2,1)S(1)} %get-tuple-element.114) | copy-start | bytes 1179652
  1559.0 81.6 %all-to-all-start.9 = ((bf16[8,5,56,1536]{3,2,1,0:T(8,128)(2,1)}), bf16[8,5,56,1536]{3,2,1,0:T(8,128)(2,1)}, u32[]{:S(2)}, u32[]{:S(2)}) async-start(bf16[8,5,56,1536]{3,2,1,0:T(8,128)(2,1)} %copy.473), calls=%async_computation.9 | async-start | bytes 13762560 | tf_op jit(solution)/shard_map/all_to_all | solution.py:127
  1640.6 81.4 %all-to-all-start.7 = ((bf16[8,5,56,1536]{3,2,1,0:T(8,128)(2,1)}), bf16[8,5,56,1536]{3,2,1,0:T(8,128)(2,1)}, u32[]{:S(2)}, u32[]{:S(2)}) async-start(bf16[8,5,56,1536]{3,2,1,0:T(8,128)(2,1)} %copy.456), calls=%async_computation.7 | async-start | bytes 13762560 | tf_op jit(solution)/shard_map/all_to_all | solution.py:127
  1722.0 81.4 %all-to-all-start = ((bf16[8,5,56,1536]{3,2,1,0:T(8,128)(2,1)}), bf16[8,5,56,1536]{3,2,1,0:T(8,128)(2,1)}, u32[]{:S(2)}, u32[]{:S(2)}) async-start(bf16[8,5,56,1536]{3,2,1,0:T(8,128)(2,1)} %bitcast.3698), calls=%async_computation | async-start | bytes 13762560 | tf_op jit(solution)/shard_map/all_to_all | solution.py:125
  1803.4 81.4 %all-to-all-start.15 = ((bf16[8,5,56,1536]{3,2,1,0:T(8,128)(2,1)}), bf16[8,5,56,1536]{3,2,1,0:T(8,128)(2,1)}, u32[]{:S(2)}, u32[]{:S(2)}) async-start(bf16[8,5,56,1536]{3,2,1,0:T(8,128)(2,1)} %copy.524), calls=%async_computation.15 | async-start | bytes 13762560 | tf_op jit(solution)/shard_map/all_to_all | solution.py:127
  1884.7 81.4 %all-to-all-start.17 = ((bf16[8,5,56,1536]{3,2,1,0:T(8,128)(2,1)}), bf16[8,5,56,1536]{3,2,1,0:T(8,128)(2,1)}, u32[]{:S(2)}, u32[]{:S(2)}) async-start(bf16[8,5,56,1536]{3,2,1,0:T(8,128)(2,1)} %copy.528), calls=%async_computation.17 | async-start | bytes 13762560 | tf_op jit(solution)/shard_map/all_to_all | solution.py:139
  1966.1 81.7 %all-to-all-start.1 = ((bf16[8,5,56,1536]{3,2,1,0:T(8,128)(2,1)}), bf16[8,5,56,1536]{3,2,1,0:T(8,128)(2,1)}, u32[]{:S(2)}, u32[]{:S(2)}) async-start(bf16[8,5,56,1536]{3,2,1,0:T(8,128)(2,1)} %copy.405), calls=%async_computation.1 | async-start | bytes 13762560 | tf_op jit(solution)/shard_map/all_to_all | solution.py:127
  1970.0 52.0 %copy-start.582 = (f32[2,64]{1,0:T(2,128)}, f32[2,64]{1,0:T(2,128)S(1)}, u32[]{:S(2)}) copy-start(f32[2,64]{1,0:T(2,128)S(1)} %fusion.1724) | copy-start | bytes 1540
  2047.8 81.5 %all-to-all-start.4 = ((bf16[8,5,56,1536]{3,2,1,0:T(8,128)(2,1)}), bf16[8,5,56,1536]{3,2,1,0:T(8,128)(2,1)}, u32[]{:S(2)}, u32[]{:S(2)}) async-start(bf16[8,5,56,1536]{3,2,1,0:T(8,128)(2,1)} %bitcast.3697), calls=%async_computation.4 | async-start | bytes 13762560 | tf_op jit(solution)/shard_map/all_to_all | solution.py:125
  2129.3 81.8 %all-to-all-start.20 = ((bf16[8,5,56,1536]{3,2,1,0:T(8,128)(2,1)}), bf16[8,5,56,1536]{3,2,1,0:T(8,128)(2,1)}, u32[]{:S(2)}, u32[]{:S(2)}) async-start(bf16[8,5,56,1536]{3,2,1,0:T(8,128)(2,1)} %bitcast.3703), calls=%async_computation.20 | async-start | bytes 13762560 | tf_op jit(solution)/shard_map/all_to_all | solution.py:137
  2254.8 81.5 %all-to-all-start.21 = ((bf16[8,5,56,1536]{3,2,1,0:T(8,128)(2,1)}), bf16[8,5,56,1536]{3,2,1,0:T(8,128)(2,1)}, u32[]{:S(2)}, u32[]{:S(2)}) async-start(bf16[8,5,56,1536]{3,2,1,0:T(8,128)(2,1)} %copy.546), calls=%async_computation.21 | async-start | bytes 13762560 | tf_op jit(solution)/shard_map/all_to_all | solution.py:139
  2336.3 81.4 %all-to-all-start.5 = ((bf16[8,5,56,1536]{3,2,1,0:T(8,128)(2,1)}), bf16[8,5,56,1536]{3,2,1,0:T(8,128)(2,1)}, u32[]{:S(2)}, u32[]{:S(2)}) async-start(bf16[8,5,56,1536]{3,2,1,0:T(8,128)(2,1)} %copy.439), calls=%async_computation.5 | async-start | bytes 13762560 | tf_op jit(solution)/shard_map/all_to_all | solution.py:127
  2417.7 81.4 %all-to-all-start.2 = ((bf16[8,5,56,1536]{3,2,1,0:T(8,128)(2,1)}), bf16[8,5,56,1536]{3,2,1,0:T(8,128)(2,1)}, u32[]{:S(2)}, u32[]{:S(2)}) async-start(bf16[8,5,56,1536]{3,2,1,0:T(8,128)(2,1)} %bitcast.3695), calls=%async_computation.2 | async-start | bytes 13762560 | tf_op jit(solution)/shard_map/all_to_all | solution.py:125
  2499.1 81.7 %all-to-all-start.18 = ((bf16[8,5,56,1536]{3,2,1,0:T(8,128)(2,1)}), bf16[8,5,56,1536]{3,2,1,0:T(8,128)(2,1)}, u32[]{:S(2)}, u32[]{:S(2)}) async-start(bf16[8,5,56,1536]{3,2,1,0:T(8,128)(2,1)} %bitcast.3702), calls=%async_computation.18 | async-start | bytes 13762560 | tf_op jit(solution)/shard_map/all_to_all | solution.py:137
  2624.4 81.9 %all-to-all-start.19 = ((bf16[8,5,56,1536]{3,2,1,0:T(8,128)(2,1)}), bf16[8,5,56,1536]{3,2,1,0:T(8,128)(2,1)}, u32[]{:S(2)}, u32[]{:S(2)}) async-start(bf16[8,5,56,1536]{3,2,1,0:T(8,128)(2,1)} %copy.537), calls=%async_computation.19 | async-start | bytes 13762560 | tf_op jit(solution)/shard_map/all_to_all | solution.py:139
  2706.3 192.2 %all-to-all-start.3 = ((bf16[8,5,56,1536]{3,2,1,0:T(8,128)(2,1)}), bf16[8,5,56,1536]{3,2,1,0:T(8,128)(2,1)}, u32[]{:S(2)}, u32[]{:S(2)}) async-start(bf16[8,5,56,1536]{3,2,1,0:T(8,128)(2,1)} %copy.422), calls=%async_computation.3 | async-start | bytes 13762560 | tf_op jit(solution)/shard_map/all_to_all | solution.py:127
  2709.9 499.2 %all-reduce.36.cloned.1.call-start = ((), (), s32[]{:S(2)}) async-start(), calls=%async_computation.32 | async-start | bytes 69206016 | tf_op jit(solution)/shard_map/psum | solution.py:150
  2756.3 36.8 %copy-start.134 = (f32[2,64,24,32]{1,3,2,0:T(8,128)}, f32[2,64,24,32]{1,3,2,0:T(8,128)S(1)}, u32[]{:S(2)}) copy-start(f32[2,64,24,32]{1,3,2,0:T(8,128)S(1)} %get-tuple-element.233) | copy-start | bytes 1179652
  2848.0 30.0 copy-start.27
  2909.7 30.1 copy-start.72
  2912.6 29.7 copy-start.69
  (708 other events, 4060.6 us)
Sparse Core Ops, SparseCore 0:
  2808.0 401.0 all-reduce.35
where the time goes:
time: 3260 us; the launch traced here: 3240 us
  matrix products  1350 us (41%)
  waiting for transfers between devices  971 us (30%)
  local copies, waits for them, and re-layouts  485 us (15%)
  other arithmetic  273 us (8%)
  starting transfers between devices  119 us (4%)
    psum x1, waiting for transfers between devices, device_fn(): dense_out = lax.psum(dense_out, 'ep')  251 us
    all_to_all x8, waiting for transfers between devices, device_fn(): recv_rows = lax.all_to_all(send_rows, 'ep', 0, 0, tiled=True)  234 us
    all_to_all x8, waiting for transfers between devices, device_fn(): recv_grad = lax.all_to_all(send_grad, 'ep', 0, 0, tiled=True)  193 us
    all_to_all x8, waiting for transfers between devices, device_fn(): lax.all_to_all(d_rows, 'ep', 0, 0, tiled=True)  152 us
    all_to_all x8, waiting for transfers between devices, device_fn(): lax.all_to_all(expert_res, 'ep', 0, 0, tiled=True)  141 us
    dot_general x8, matrix products, expert_backward(): jnp.einsum('nxcf,nxcd->xfd', inner, d_out, preferred_element_type=jnp.flo...  113 us
    dot_general x8, matrix products, expert_backward(): jnp.einsum('nxcd,xfd->nxcf', d_out, e_down, preferred_element_type=jnp.fl...  113 us
    dot_general x8, matrix products, expert_backward(): jnp.einsum('nxcd,nxcf->xdf', rows_in, d_up, preferred_element_type=jnp.fl...  107 us
  transfers between devices with their start and end apart: 33, of which 31 were waited for; matrix products, arithmetic and copies ran while one was open for 59% of the time, Pallas kernels for 0%

commit v1 on v0

v1 whole, which is shorter than its diff:
```python
import functools

import jax
import jax.numpy as jnp
from jax import lax
from jax.experimental import pallas as pl
from jax.experimental.pallas import tpu as pltpu
from jax.sharding import PartitionSpec as P

EPS = 1e-6
ROPE_BASE = 10000.0
CAP_FACTOR = 2
F32 = jnp.float32
BF16 = jnp.bfloat16
KEY_STRIDE = 128
VMEM_BIG = 66_000_000


def capacity_of(tokens, top_k, n_exp):
    return 8 * ((CAP_FACTOR * tokens * top_k + 8 * n_exp - 1) // (8 * n_exp))


def dot_nn(lhs, rhs):
    return lax.dot_general(lhs, rhs, (((1,), (0,)), ((), ())), preferred_element_type=F32)


def dot_nt(lhs, rhs):
    return lax.dot_general(lhs, rhs, (((1,), (1,)), ((), ())), preferred_element_type=F32)


def dot_tn(lhs, rhs):
    return lax.dot_general(lhs, rhs, (((0,), (0,)), ((), ())), preferred_element_type=F32)


def rms_norm(values, gain_w):
    vals_f = values.astype(F32)
    inv_rms = lax.rsqrt(jnp.mean(vals_f * vals_f, axis=-1, keepdims=True) + EPS)
    return (vals_f * inv_rms * gain_w.astype(F32)).astype(BF16)


def rms_norm_grad(values, gain_w, d_out):
    vals_f = values.astype(F32)
    inv_rms = lax.rsqrt(jnp.mean(vals_f * vals_f, axis=-1, keepdims=True) + EPS)
    unit = vals_f * inv_rms
    d_f = d_out.astype(F32)
    d_gain = jnp.sum(d_f * unit, axis=0)
    d_unit = d_f * gain_w.astype(F32)
    d_vals = inv_rms * (d_unit - unit * jnp.mean(d_unit * unit, axis=-1, keepdims=True))
    return d_vals.astype(BF16), d_gain


def rope_rotate(tensor, cos_t, sin_t):
    half_dim = tensor.shape[-1] // 2
    tens_f = tensor.astype(F32)
    first_half = tens_f[..., :half_dim]
    second_half = tens_f[..., half_dim:]
    return jnp.concatenate([first_half * cos_t - second_half * sin_t, second_half * cos_t + first_half * sin_t], axis=-1).astype(BF16)


def attend(query, key, value, seq_len, head_dim):
    tokens = query.shape[0]
    n_seq = tokens // seq_len
    kv_heads = key.shape[1] // head_dim
    q_group = query.shape[1] // key.shape[1]
    position = jnp.arange(seq_len, dtype=F32)
    inv_freq = ROPE_BASE ** (-jnp.arange(head_dim // 2, dtype=F32) / (head_dim // 2))
    angle_t = position[:, None] * inv_freq[None, :]
    cos_t = jnp.cos(angle_t)[:, None, :]
    sin_t = jnp.sin(angle_t)[:, None, :]
    query_heads = rope_rotate(query.reshape(n_seq, seq_len, kv_heads * q_group, head_dim), cos_t, sin_t)
    query_heads = query_heads.reshape(n_seq, seq_len, kv_heads, q_group, head_dim)
    key_heads = rope_rotate(key.reshape(n_seq, seq_len, kv_heads, head_dim), cos_t, sin_t)
    value_heads = value.reshape(n_seq, seq_len, kv_heads, head_dim)
    scores = jnp.einsum('nqhgk,nshk->nhgqs', query_heads, key_heads, preferred_element_type=F32) * head_dim ** -0.5
    causal = jnp.arange(seq_len)[:, None] >= jnp.arange(seq_len)[None, :]
    attn_prob = jax.nn.softmax(jnp.where(causal, scores, -1e30), axis=-1).astype(BF16)
    mixed = jnp.einsum('nhgqs,nshk->nqhgk', attn_prob, value_heads, preferred_element_type=F32).astype(BF16)
    return mixed.reshape(tokens, kv_heads * q_group * head_dim)


def choice_keys(choice_ids, n_exp):
    n_slots, top_k, tokens = choice_ids.shape
    same = choice_ids[:, None, :, :] == jnp.arange(n_exp)[None, :, None, None]
    count = jnp.sum(same, axis=2, dtype=F32)
    before = (jnp.arange(tokens)[:, None] < jnp.arange(tokens)[None, :]).astype(BF16)
    prefix = jnp.einsum('set,tu->seu', count.astype(BF16), before, preferred_element_type=F32)
    rank = jnp.sum(jnp.where(same, prefix[:, :, None, :], 0.0), axis=1)
    earlier = jnp.arange(top_k)[:, None] > jnp.arange(top_k)[None, :]
    repeat = (choice_ids[:, :, None, :] == choice_ids[:, None, :, :]) & earlier[None, :, :, None]
    rank = rank + jnp.sum(repeat, axis=2, dtype=F32)
    return choice_ids.astype(F32) * KEY_STRIDE + rank


def expert_kernel(n_pairs, local_e, cap, key_ref, gate_ref, u_ref, dy_ref, wg_ref, wu_ref, wd_ref,
                  y_ref, du_ref, rows_ref, drows_ref, dgate_ref, dup_ref, inner_ref,
                  pick, pick_g, buf_u, buf_d):
    step = pl.program_id(1)
    tokens = u_ref.shape[1]
    d_model = u_ref.shape[2]
    top_k = key_ref.shape[2]
    pair_rows = 2 * cap

    @pl.when(step < n_pairs)
    def _gather():
        pair = step
        for exp in range(local_e):
            for src in range(2):
                row = lax.broadcasted_iota(jnp.int32, (pair_rows, tokens), 0).astype(F32) + (exp * KEY_STRIDE - src * cap)
                chosen = jnp.zeros((pair_rows, tokens), F32)
                weight = jnp.zeros((pair_rows, tokens), F32)
                for choice in range(top_k):
                    hit = key_ref[src, 0, choice:choice + 1, :] == row
                    chosen = jnp.where(hit, 1.0, chosen)
                    weight = jnp.where(hit, gate_ref[src, 0, choice:choice + 1, :], weight)
                pick[pair, pl.ds(exp * pair_rows, pair_rows), src * tokens:(src + 1) * tokens] = chosen.astype(BF16)
                pick_g[pair, pl.ds(exp * pair_rows, pair_rows), src * tokens:(src + 1) * tokens] = weight.astype(BF16)
        u_all = u_ref[...].reshape(2 * tokens, d_model)
        dy_all = dy_ref[...].reshape(2 * tokens, d_model)
        buf_u[pair] = dot_nn(pick[pair], u_all).astype(BF16)
        buf_d[pair] = dot_nn(pick_g[pair], dy_all).astype(BF16)

    @pl.when((step >= n_pairs) & (step < n_pairs + local_e))
    def _experts():
        exp = step - n_pairs
        start = pl.multiple_of(exp * pair_rows, 16)
        rows = buf_u[:, pl.ds(start, pair_rows), :].reshape(n_pairs * pair_rows, d_model)
        d_out = buf_d[:, pl.ds(start, pair_rows), :].reshape(n_pairs * pair_rows, d_model)
        rows_ref[0, 0] = rows
        drows_ref[0, 0] = d_out
        gate_f = dot_nn(rows, wg_ref[0]).astype(BF16).astype(F32)
        up_f = dot_nn(rows, wu_ref[0]).astype(BF16).astype(F32)
        sig_gate = jax.nn.sigmoid(gate_f)
        silu_gate = gate_f * sig_gate
        inner = (silu_gate * up_f).astype(BF16)
        inner_ref[0, 0] = inner
        d_inner = dot_nt(d_out, wd_ref[0]).astype(BF16).astype(F32)
        d_gate = (d_inner * up_f * sig_gate * (1.0 + gate_f * (1.0 - sig_gate))).astype(BF16)
        d_up = (d_inner * silu_gate).astype(BF16)
        dgate_ref[0, 0] = d_gate
        dup_ref[0, 0] = d_up
        result = dot_nn(inner, wd_ref[0]).astype(BF16)
        buf_u[:, pl.ds(start, pair_rows), :] = result.reshape(n_pairs, pair_rows, d_model)
        from_gate = dot_nt(d_gate, wg_ref[0]).astype(BF16).astype(F32)
        from_up = dot_nt(d_up, wu_ref[0]).astype(BF16).astype(F32)
        d_rows = (from_gate + from_up).astype(BF16)
        buf_d[:, pl.ds(start, pair_rows), :] = d_rows.reshape(n_pairs, pair_rows, d_model)

    @pl.when(step >= n_pairs + local_e)
    def _combine():
        pair = step - (n_pairs + local_e)
        y_ref[...] = dot_tn(pick_g[pair], buf_u[pair]).reshape(2, tokens, d_model)
        du_ref[...] = dot_tn(pick[pair], buf_d[pair]).reshape(2, tokens, d_model)


def expert_pass(keys, gates, u_all, dy_all, e_gate, e_up, e_down, cap, tokens):
    n_dev, n_slots, top_k, _ = keys.shape
    local_e, d_model, d_ff = e_gate.shape
    n_pairs = n_dev // 2
    exp_rows = n_dev * cap
    all_rows = n_pairs * local_e * 2 * cap
    last = n_pairs + local_e

    def pair_in(slot, step):
        return jnp.minimum(step, n_pairs - 1)

    def expert_of(slot, step):
        return jnp.clip(step - n_pairs, 0, local_e - 1)

    def pair_out(slot, step):
        return jnp.maximum(step - last, 0)

    route_spec = pl.BlockSpec((2, 1, top_k, tokens), lambda slot, step: (pair_in(slot, step), slot, 0, 0))
    token_in = pl.BlockSpec((2, tokens, d_model), lambda slot, step: (pair_in(slot, step), slot, 0))
    token_out = pl.BlockSpec((2, tokens, d_model), lambda slot, step: (pair_out(slot, step), slot, 0))
    wide = pl.BlockSpec((1, d_model, d_ff), lambda slot, step: (expert_of(slot, step), 0, 0))
    tall = pl.BlockSpec((1, d_ff, d_model), lambda slot, step: (expert_of(slot, step), 0, 0))
    save_d = pl.BlockSpec((1, 1, exp_rows, d_model), lambda slot, step: (slot, expert_of(slot, step), 0, 0))
    save_f = pl.BlockSpec((1, 1, exp_rows, d_ff), lambda slot, step: (slot, expert_of(slot, step), 0, 0))
    token_sum = jax.ShapeDtypeStruct((n_dev, n_slots * tokens, d_model), F32)
    saved_d = jax.ShapeDtypeStruct((n_slots, local_e, exp_rows, d_model), BF16)
    saved_f = jax.ShapeDtypeStruct((n_slots, local_e, exp_rows, d_ff), BF16)
    flops = n_slots * all_rows * (12 * d_model * d_ff + 8 * 2 * tokens * d_model)
    return pl.pallas_call(
        functools.partial(expert_kernel, n_pairs, local_e, cap),
        grid=(n_slots, last + n_pairs),
        in_specs=[route_spec, route_spec, token_in, token_in, wide, wide, tall],
        out_specs=[token_out, token_out, save_d, save_d, save_f, save_f, save_f],
        out_shape=[token_sum, token_sum, saved_d, saved_d, saved_f, saved_f, saved_f],
        scratch_shapes=[
            pltpu.VMEM((n_pairs, local_e * 2 * cap, 2 * tokens), BF16),
            pltpu.VMEM((n_pairs, local_e * 2 * cap, 2 * tokens), BF16),
            pltpu.VMEM((n_pairs, local_e * 2 * cap, d_model), BF16),
            pltpu.VMEM((n_pairs, local_e * 2 * cap, d_model), BF16),
        ],
        compiler_params=pltpu.CompilerParams(vmem_limit_bytes=VMEM_BIG, dimension_semantics=('arbitrary', 'arbitrary')),
        cost_estimate=pl.CostEstimate(flops=flops, bytes_accessed=n_slots * 60_000_000, transcendentals=0),
        name='expert_pass',
    )(keys, gates, u_all, dy_all, e_gate, e_up, e_down)


def expert_grad_kernel(rows_ref, drows_ref, dgate_ref, dup_ref, inner_ref, g_gate_ref, g_up_ref, g_down_ref):
    part = pl.program_id(1)
    n_slots, _, n_rows, d_model = rows_ref.shape
    d_ff = dgate_ref.shape[3]
    rows = rows_ref[...].reshape(n_slots * n_rows, d_model)
    d_out = drows_ref[...].reshape(n_slots * n_rows, d_model)
    d_gate = dgate_ref[...].reshape(n_slots * n_rows, d_ff)
    d_up = dup_ref[...].reshape(n_slots * n_rows, d_ff)
    inner = inner_ref[...].reshape(n_slots * n_rows, d_ff)

    @pl.when(part == 0)
    def _first():
        g_gate_ref[0] = dot_tn(rows, d_gate)
        g_up_ref[0] = dot_tn(rows, d_up)
        g_down_ref[0] = dot_tn(inner, d_out)

    @pl.when(part > 0)
    def _rest():
        g_gate_ref[0] += dot_tn(rows, d_gate)
        g_up_ref[0] += dot_tn(rows, d_up)
        g_down_ref[0] += dot_tn(inner, d_out)


def expert_grads(rows, d_rows, d_gate, d_up, inner, per_step):
    n_slots, local_e, n_rows, d_model = rows.shape
    d_ff = d_gate.shape[3]
    parts = n_slots // per_step
    in_d = pl.BlockSpec((per_step, 1, n_rows, d_model), lambda exp, part: (part, exp, 0, 0))
    in_f = pl.BlockSpec((per_step, 1, n_rows, d_ff), lambda exp, part: (part, exp, 0, 0))
    wide = pl.BlockSpec((1, d_model, d_ff), lambda exp, part: (exp, 0, 0))
    tall = pl.BlockSpec((1, d_ff, d_model), lambda exp, part: (exp, 0, 0))
    flops = 6 * n_slots * local_e * n_rows * d_model * d_ff
    return pl.pallas_call(
        expert_grad_kernel,
        grid=(local_e, parts),
        in_specs=[in_d, in_d, in_f, in_f, in_f],
        out_specs=[wide, wide, tall],
        out_shape=[jax.ShapeDtypeStruct((local_e, d_model, d_ff), F32)] * 2 + [jax.ShapeDtypeStruct((local_e, d_ff, d_model), F32)],
        compiler_params=pltpu.CompilerParams(vmem_limit_bytes=VMEM_BIG, dimension_semantics=('arbitrary', 'arbitrary')),
        cost_estimate=pl.CostEstimate(flops=flops, bytes_accessed=250_000_000, transcendentals=0),
        name='expert_grads',
    )(rows, d_rows, d_gate, d_up, inner)


def solution(mesh):
    n_ep = mesh.shape['ep']

    def device_fn(x_in, dy_in, expert_id, gate_vals, norm_attn, w_query, w_key, w_value, w_out, norm_ffn, s_gate, s_up, s_down, e_gate, e_up, e_down):
        n_slots, n_seq, seq_len, d_model = x_in.shape
        heads, head_dim = w_query.shape[2:]
        kv_heads = w_key.shape[2]
        top_k = expert_id.shape[-1]
        local_e = e_gate.shape[1]
        n_exp = local_e * n_ep
        tokens = n_seq * seq_len
        cap = capacity_of(tokens, top_k, n_exp)
        all_tok = n_slots * tokens
        x = x_in.reshape(all_tok, d_model)
        dy = dy_in.reshape(all_tok, d_model)
        norm_a, norm_f = norm_attn[0], norm_ffn[0]
        q_dim, kv_dim = heads * head_dim, kv_heads * head_dim
        wt_q = jnp.transpose(w_query[0], (1, 2, 0)).reshape(q_dim, d_model)
        wt_k = jnp.transpose(w_key[0], (1, 2, 0)).reshape(kv_dim, d_model)
        wt_v = jnp.transpose(w_value[0], (1, 2, 0)).reshape(kv_dim, d_model)
        wo = w_out[0].reshape(q_dim, d_model)

        ids = jnp.transpose(expert_id[:, 0], (0, 3, 1, 2)).reshape(n_slots, top_k, tokens)
        gates = jnp.transpose(gate_vals[:, 0], (0, 3, 1, 2)).reshape(n_slots, top_k, tokens).astype(F32)
        table = jnp.stack([choice_keys(ids, n_exp), gates])
        table = lax.all_gather(table, 'ep', axis=0, tiled=False)
        first_key = (lax.axis_index('ep') * (local_e * KEY_STRIDE)).astype(F32)
        keys_all = table[:, 0] - first_key
        gates_all = table[:, 1]

        dy_all = lax.all_gather(dy, 'ep', axis=0, tiled=False)

        normed = rms_norm(x, norm_a)
        query = dot_nt(normed, wt_q).astype(BF16)
        key = dot_nt(normed, wt_k).astype(BF16)
        value = dot_nt(normed, wt_v).astype(BF16)
        mixed, attend_pull = jax.vjp(functools.partial(attend, seq_len=seq_len, head_dim=head_dim), query, key, value)
        hidden = (x.astype(F32) + dot_nn(mixed, wo)).astype(BF16)
        u = rms_norm(hidden, norm_f)
        u_all = lax.all_gather(u, 'ep', axis=0, tiled=False)

        y_part, du_part, rows, d_rows, x_dgate, x_dup, x_inner = expert_pass(
            keys_all, gates_all, u_all, dy_all, e_gate[0], e_up[0], e_down[0], cap, tokens)
        routed = lax.psum_scatter(y_part, 'ep', scatter_dimension=0, tiled=False)
        d_routed = lax.psum_scatter(du_part, 'ep', scatter_dimension=0, tiled=False).astype(BF16)
        g_e_gate, g_e_up, g_e_down = expert_grads(rows, d_rows, x_dgate, x_dup, x_inner, 2)

        gate_f = dot_nn(u, s_gate[0]).astype(BF16).astype(F32)
        up_f = dot_nn(u, s_up[0]).astype(BF16).astype(F32)
        sig_gate = jax.nn.sigmoid(gate_f)
        silu_gate = gate_f * sig_gate
        inner = (silu_gate * up_f).astype(BF16)
        shared = dot_nn(inner, s_down[0])
        y = (hidden.astype(F32) + shared + routed).astype(BF16)
        d_inner = dot_nt(dy, s_down[0]).astype(BF16).astype(F32)
        d_gate = (d_inner * up_f * sig_gate * (1.0 + gate_f * (1.0 - sig_gate))).astype(BF16)
        d_up = (d_inner * silu_gate).astype(BF16)
        d_shared = dot_nt(d_gate, s_gate[0]).astype(BF16).astype(F32) + dot_nt(d_up, s_up[0]).astype(BF16).astype(F32)
        g_s_gate = dot_tn(u, d_gate)
        g_s_up = dot_tn(u, d_up)
        g_s_down = dot_tn(inner, dy)

        d_u = (d_routed.astype(F32) + d_shared.astype(BF16).astype(F32)).astype(BF16)
        d_hidden_u, g_norm_f = rms_norm_grad(hidden, norm_f, d_u)
        d_hidden = (dy.astype(F32) + d_hidden_u.astype(F32)).astype(BF16)
        d_mixed = dot_nt(d_hidden, wo).astype(BF16)
        g_out = dot_tn(mixed, d_hidden)
        d_query, d_key, d_value = attend_pull(d_mixed)
        g_q = dot_tn(d_query, normed)
        g_k = dot_tn(d_key, normed)
        g_v = dot_tn(d_value, normed)
        d_normed = (dot_nn(d_query, wt_q) + dot_nn(d_key, wt_k) + dot_nn(d_value, wt_v)).astype(BF16)
        d_x_norm, g_norm_a = rms_norm_grad(x, norm_a, d_normed)
        dx = (d_hidden.astype(F32) + d_x_norm.astype(F32)).astype(BF16)

        grads = lax.psum([g_q, g_k, g_v, g_out, g_s_gate, g_s_up, g_s_down, g_norm_a, g_norm_f], 'ep')
        g_q, g_k, g_v, g_out, g_s_gate, g_s_up, g_s_down, g_norm_a, g_norm_f = grads
        return (
            y.reshape(x_in.shape), dx.reshape(x_in.shape), g_norm_a[None],
            jnp.transpose(g_q.reshape(heads, head_dim, d_model), (2, 0, 1))[None],
            jnp.transpose(g_k.reshape(kv_heads, head_dim, d_model), (2, 0, 1))[None],
            jnp.transpose(g_v.reshape(kv_heads, head_dim, d_model), (2, 0, 1))[None],
            g_out.reshape(heads, head_dim, d_model)[None], g_norm_f[None], g_s_gate[None], g_s_up[None], g_s_down[None],
            g_e_gate[None], g_e_up[None], g_e_down[None],
        )

    tok_spec = P(None, ('dp', 'ep'), None, None)
    route_spec = P(None, None, ('dp', 'ep'), None, None)
    rep_spec = P()
    exp_spec = P(None, 'ep', None, None)
    vec_grad = P('dp', None)
    mat_grad = P('dp', None, None)
    head_grad = P('dp', None, None, None)
    exp_grad = P('dp', 'ep', None, None)
    in_specs = (tok_spec, tok_spec, route_spec, route_spec) + (rep_spec,) * 9 + (exp_spec,) * 3
    out_specs = (tok_spec, tok_spec, vec_grad, head_grad, head_grad, head_grad, head_grad, vec_grad, mat_grad, mat_grad, mat_grad, exp_grad, exp_grad, exp_grad)
    return jax.shard_map(device_fn, mesh=mesh, in_specs=in_specs, out_specs=out_specs, check_vma=False)
```

time: 3260 us -> 1720 us (0.53)
  matrix products: 1350 us -> 185 us
  Pallas kernels: 0 us -> 463 us
  local copies, waits for them, and re-layouts: 485 us -> 149 us
  other arithmetic: 273 us -> 74.8 us
  waiting for transfers between devices: 971 us -> 785 us
  starting transfers between devices: 119 us -> 0.37 us
    dot_general x296 -> x28, matrix products: 1350 us -> 185 us  [the longest x3 46 us: attend(): jnp.einsum('nqhgk,nshk->nhgqs', query_heads, key_heads, preferred_element...]
    all_to_all x32 -> x0, waiting for transfers between devices: 720 us -> none  [the longest x8 234 us: device_fn(): recv_rows = lax.all_to_all(send_rows, 'ep', 0, 0, tiled=True)]
    pallas_call x0 -> x2, Pallas kernels: none -> 463 us  [the longest x1 338 us: expert_pass(): pl.pallas_call(functools.partial(expert_kernel, n_pairs, local_e, cap), g...]
    reduce_scatter x0 -> x2, waiting for transfers between devices: none -> 250 us  [the longest x1 250 us: device_fn(): lax.psum_scatter(du_part, 'ep', scatter_dimension=0, tiled=False)]
    all_gather x0 -> x2, waiting for transfers between devices: none -> 224 us  [the longest x1 121 us: device_fn(): dy_all = lax.all_gather(dy, 'ep', axis=0, tiled=False)]
    gather x16 -> x0, local copies, waits for them, and re-layouts: 181 us -> none  [the longest x8 90.7 us: device_fn(): returned[position]]
    all_to_all x32 -> x0, starting transfers between devices: 119 us -> none  [the longest x8 30.2 us: device_fn(): recv_rows = lax.all_to_all(send_rows, 'ep', 0, 0, tiled=True)]
    another operation x23 -> x3, other arithmetic: 103 us -> 13.9 us
  transfers between devices with their start and end apart: 33 -> 5, of which waited for: 31 -> 4; matrix products, arithmetic and copies ran while one was open for 59% -> 14% of each run, Pallas kernels for 0% -> 7%
where the time goes in v1:
time: 1720 us; the launch traced here: 1710 us
  waiting for transfers between devices  785 us (46%)
  Pallas kernels  463 us (27%)
  matrix products  185 us (11%)
  local copies, waits for them, and re-layouts  149 us (9%)
  other arithmetic  74.8 us (4%)
  blocking collectives  41.4 us (2%)
    pallas_call x1, Pallas kernels, expert_pass(): pl.pallas_call(functools.partial(expert_kernel, n_pairs, local_e, cap), g...  338 us
    psum x1, waiting for transfers between devices, device_fn(): lax.psum([g_q, g_k, g_v, g_out, g_s_gate, g_s_up, g_s_down, g_norm_a, g_n...  310 us
    reduce_scatter x1, waiting for transfers between devices, device_fn(): lax.psum_scatter(du_part, 'ep', scatter_dimension=0, tiled=False)  250 us
    pallas_call x1, Pallas kernels, expert_grads(): pl.pallas_call(expert_grad_kernel, grid=(local_e, parts), in_specs=[in_d,...  125 us
    all_gather x1, waiting for transfers between devices, device_fn(): dy_all = lax.all_gather(dy, 'ep', axis=0, tiled=False)  121 us
    all_gather x1, waiting for transfers between devices, device_fn(): u_all = lax.all_gather(u, 'ep', axis=0, tiled=False)  102 us
    unnamed x143, local copies, waits for them, and re-layouts  52.7 us
    dot_general x3, matrix products, attend(): jnp.einsum('nqhgk,nshk->nhgqs', query_heads, key_heads, preferred_element...  46 us
  transfers between devices with their start and end apart: 5, of which 4 were waited for; matrix products, arithmetic and copies ran while one was open for 14% of the time, Pallas kernels for 7%

profile of v1, /device:TPU:0, one launch (start us, length us, event | category | flops | bytes accessed | tf_op | source)
XLA Modules:
  0.0 1713.9 jit_solution(1809220881130117612)
XLA Ops:
  8.2 2.7 fusion.30
  13.4 1.8 fusion.76
  15.2 2.5 reshape.333
  17.6 8.2 fusion.98
  26.0 9.3 fusion.38
  35.4 10.0 reshape.334
  45.3 10.6 subtract_convert_fusion
  55.9 4.5 copy.94
  60.5 4.7 copy.95
  65.5 3.2 subtract_convert_fusion.1
  68.7 17.5 %fusion.7 = (f32[16,8,3,64]{3,2,1,0:T(4,128)S(1)}, f32[16,8,64,64,3]{3,2,4,1,0:T(8,128)}) fusion(pred[64,64]{0,1:T(8,128)(4,1)S(1)} %iota_compare_fusion.3, bf16[16,64,8,3,32]{4,1,3,2,0:T(8,128)(2,1)} %bitcast.236, bf16[16,64,8,3,32]{4,1,3,2,0:T(8,128)(2,1)} %bitcast.232, bf16[16,64,8,32]{3,1,2,0:T(8,128)(2,1)} %get-tuple-element.54, ...), kind=kOutput, calls=%fused_computation.17 | convolution fusion | flops 214409216 | bytes 10588160 | tf_op jit(solution)/shard_map/jvp(nqhgk,nshk->nhgqs)/dot_general | solution.py:74
  86.3 8.7 fusion.15
  95.0 5.1 divide_convert_fusion
  100.2 1.8 convolution_convert_fusion.5
  103.1 5.4 convert_bitcast_fusion.1
  108.5 8.4 copy.98
  117.0 9.5 reshape.320
  126.5 9.1 fusion.25
  137.3 2.4 fusion.22
  141.9 18.3 %all-gather = f32[16,8,8,128]{3,2,1,0:T(8,128)S(1)} all-gather(f32[2,8,8,128]{3,2,1,0:T(8,128)S(1)} %pad_maximum_fusion.3), channel_id=2, replica_groups=mesh['dp'=1,'ep'=8] {'ep'}, dimensions={0}, use_global_device_ids=true | all-gather | bytes 589824 | tf_op jit(solution)/shard_map/all_gather | solution.py:270
  161.7 102.2 %all-gather.7.cloned.1.call-done = bf16[8192,1536]{1,0:T(8,128)(2,1)} async-done(((bf16[1024,1536]{1,0:T(8,128)(2,1)}), bf16[8192,1536]{1,0:T(8,128)(2,1)}) %all-gather.7.cloned.1.call-update) | async-done | bytes 25165840 | tf_op jit(solution)/shard_map/all_gather | solution.py:284
  263.9 121.5 %all-gather.5.cloned.1.call-done.dy_ref = bf16[8,1024,1536]{2,1,0:T(8,128)(2,1)} async-done(((bf16[1,1024,1536]{2,1,0:T(8,128)(2,1)}), bf16[8,1024,1536]{2,1,0:T(8,128)(2,1)}) %all-gather.5.cloned.1.call-update) | async-done | bytes 25165840 | tf_op jit(solution)/shard_map/all_gather | solution.py:275
  385.4 337.9 %expert_pass.1 = (f32[8,1024,1536]{2,1,0:T(8,128)}, f32[8,1024,1536]{2,1,0:T(8,128)}, bf16[8,5,448,1536]{3,2,1,0:T(8,128)(2,1)}, bf16[8,5,448,1536]{3,2,1,0:T(8,...) custom-call(f32[8,8,8,128]{3,2,1,0:T(8,128)} %fusion.79.key_ref, ...), custom_call_target="tpu_custom_call" | custom-call | flops 225485783040 | bytes 480000000 | tf_op jit(solution)/shard_map/expert_pass/pallas_call | solution.py:183
  725.3 3.3 fusion.67
  731.4 1.8 fusion.73
  733.2 3.6 convolution_convert_fusion.1
  736.8 3.5 convolution_bitcast_fusion
  740.4 3.6 convolution_bitcast_fusion.1
  744.0 3.8 convolution_bitcast_fusion.2
  747.7 250.2 %reduce-scatter.5.cloned.1.call-done = f32[1,1024,1536]{2,1,0:T(8,128)} async-done(((f32[8,1024,1536]{2,1,0:T(8,128)}), f32[1,1024,1536]{2,1,0:T(8,128)}) %reduce-scatter.5.cloned.1.call-update) | async-done | bytes 6291472 | tf_op jit(solution)/shard_map/reduce_scatter | solution.py:289
  997.9 10.5 fusion.24
  1008.4 2.6 add_convert_fusion.4
  1012.6 7.6 convolution_convert_fusion
  1020.3 2.9 copy.104
  1023.1 9.4 reshape.323
  1032.5 15.7 fusion.6
  1048.4 14.9 convert_bitcast_fusion.2
  1063.3 4.8 multiply_add_fusion.3
  1069.3 3.1 copy.112
  1072.4 4.0 reshape.325
  1076.4 13.5 convert_convert_fusion
  1090.0 11.9 fusion.97
  1101.9 9.6 copy.136
  1111.5 9.6 copy.137
  1121.1 14.5 multiply_add_fusion.1
  1135.6 9.6 add_convert_fusion
  1145.2 9.4 reshape.324
  1154.6 8.2 fusion.55
  1162.8 2.8 copy.115
  1165.6 3.2 reshape.326
  1168.8 5.8 fusion.102
  1174.6 3.6 fusion.103
  1178.2 7.5 fusion.104
  1185.7 8.0 fusion.101
  1194.4 124.8 %expert_grads.1 = (f32[5,1536,512]{2,1,0:T(8,128)}, f32[5,1536,512]{2,1,0:T(8,128)}, f32[5,512,1536]{2,1,0:T(8,128)}) custom-call(bf16[8,5,448,1536]{3,2,1,0:T(8,128)(2,1)} %get-tuple-element.26.rows_ref, bf16[8,5,448,1536]{3,2,1,0:T(8,128)(2,1)} %get-tuple-element.27.drows_ref, bf16[8,5,448,512]{3,2,1,0:T(8,128)(2,1)} %get-tuple-element.28.dgate_ref, ...), custom_call_target="tpu_custom_call" | custom-call | flops 84557168640 | bytes 250000000 | tf_op jit(solution)/shard_map/expert_grads/pallas_call | solution.py:233
  1319.2 3.7 fusion.100
  1323.0 7.1 fusion.99
  1330.1 4.1 fusion.21
  1334.2 23.1 %all-reduce.4 = (f32[1,1536]{1,0:T(1,128)}, f32[1,1536]{1,0:T(1,128)}) all-reduce(f32[1,1536]{1,0:T(1,128)S(1)} %broadcast_in_dim.109, f32[1,1536]{1,0:T(1,128)S(1)} %broadcast_in_dim.113), channel_id=1, replica_groups=mesh['dp'=1,'ep'=8] {'ep'}, use_global_device_ids=true, to_apply=%region_13.14 | all-reduce | flops 3072 | bytes 24576 | tf_op jit(solution)/shard_map/psum | solution.py:320
  1357.2 5.2 add_convert_fusion.2
  1362.4 8.6 fusion.27
  1371.0 310.2 %all-reduce.8.cloned.1.call-done = (f32[1,1536,24,64]{1,3,2,0:T(8,128)}, f32[1,1536,8,64]{1,3,2,0:T(8,128)}, f32[1,1536,8,64]{1,3,2,0:T(8,128)}, f32[1,24,64,153...) async-done(((f32[1,1536,24,64]{1,3,2,0:T(8,128)}, f32[1,1536,8,64]{1,3,2,0:T(8,128)}, f32[1,1536,8,64]{1,3,2,0:T(8,128)}, ...) | async-done | bytes 34603024 | tf_op jit(solution)/shard_map/psum | solution.py:320
  1681.2 9.3 copy.167
  1695.2 4.2 copy.170
  (188 shorter events, 31.2 us)
Async XLA Ops:
  7.2 3.7 copy-start.1
  7.2 256.7 %all-gather.7.cloned.1.call-start = ((), (), s32[]{:S(2)}) async-start(), calls=%async_computation.5 | async-start | bytes 28311552 | tf_op jit(solution)/shard_map/all_gather | solution.py:284
  7.3 87.7 %copy-start.45 = (pred[64,64]{0,1:T(8,128)(4,1)}, pred[64,64]{0,1:T(8,128)(4,1)S(1)}, u32[]{:S(2)}) copy-start(pred[64,64]{0,1:T(8,128)(4,1)S(1)} %iota_compare_fusion.3) | copy-start | bytes 12292
  8.1 3.5 copy-start.43
  8.2 5.2 copy-start.57
  11.7 1.7 copy-start.18
  17.6 8.4 copy-start.19
  26.0 39.1 %copy-start.37 = (f32[64,32]{1,0:T(8,128)}, f32[64,32]{1,0:T(8,128)S(1)}, u32[]{:S(2)}) copy-start(f32[64,32]{1,0:T(8,128)S(1)} %get-tuple-element.59) | copy-start | bytes 24580
  26.0 39.1 %copy-start.39 = (f32[64,32]{1,0:T(8,128)}, f32[64,32]{1,0:T(8,128)S(1)}, u32[]{:S(2)}) copy-start(f32[64,32]{1,0:T(8,128)S(1)} %get-tuple-element.60) | copy-start | bytes 24580
  60.5 4.7 copy-start.4
  60.5 5.0 copy-start.5
  68.7 17.5 %copy-start.14 = (bf16[16,64,8,32]{3,1,2,0:T(8,128)(2,1)}, bf16[16,64,8,32]{3,1,2,0:T(8,128)(2,1)S(1)}, u32[]{:S(2)}) copy-start(bf16[16,64,8,32]{3,1,2,0:T(8,128)(2,1)S(1)} %get-tuple-element.53) | copy-start | bytes 1572868
  86.2 8.7 copy-start.30
  86.2 8.7 copy-start
  95.0 5.2 copy-start.32
  95.0 5.2 copy-start.20
  95.0 5.2 copy-start.34
  103.1 5.4 copy-start.13
  116.9 9.5 copy-start.2
  126.5 9.1 copy-start.55
  135.6 1.7 copy-start.9
  139.7 245.6 %all-gather.5.cloned.1.call-start = ((), (), s32[]{:S(2)}) async-start(), calls=%async_computation.2 | async-start | bytes 28311552 | tf_op jit(solution)/shard_map/all_gather | solution.py:275
  140.5 857.4 %reduce-scatter.5.cloned.1.call-start = ((), (), s32[]{:S(2)}) async-start(), calls=%async_computation.4 | async-start | bytes 56623104 | tf_op jit(solution)/shard_map/reduce_scatter | solution.py:289
  723.2 639.2 %reduce-scatter.3.cloned.1.call-start = ((), (), s32[]{:S(2)}) async-start(), calls=%async_computation.3 | async-start | bytes 56623104 | tf_op jit(solution)/shard_map/reduce_scatter | solution.py:288
  723.3 2.0 copy-start.7
  723.8 957.4 %all-reduce.8.cloned.1.call-start = ((), (), s32[]{:S(2)}) async-start(), calls=%async_computation.6 | async-start | bytes 69206016 | tf_op jit(solution)/shard_map/psum | solution.py:320
  725.3 3.3 copy-start.8
  725.3 3.4 copy-start.56
  728.6 15.3 copy-start.59
  728.6 2.3 copy-start.6
  728.7 2.7 copy-start.58
  730.5 13.5 copy-start.60
  733.2 10.7 copy-start.61
  744.0 254.0 %copy-start.48 = (f32[1536]{0:T(1024)S(1)}, f32[1536]{0:T(1024)}, u32[]{:S(2)}) copy-start(f32[1536]{0:T(1024)} %copy-done.47) | copy-start | bytes 18436
  744.0 254.0 %copy-start.52 = (f32[1024]{0:T(1024)S(1)}, f32[1024]{0:T(1024)}, u32[]{:S(2)}) copy-start(f32[1024]{0:T(1024)} %copy-done.51) | copy-start | bytes 12292
  997.9 10.5 copy-start.10
  1023.1 9.4 copy-start.31
  1023.1 9.4 copy-start.41
  1023.1 9.4 copy-start.46
  1023.1 25.2 %slice-start = ((s8[6291456]{0:T(1024)(128)(4,1)}), s8[2097152]{0:T(1024)(128)(4,1)S(1)}, s32[]{:S(2)}) async-start(s8[6291456]{0:T(1024)(128)(4,1)} %bitcast.233), calls=%async_computation.7 | async-start | bytes 4194304
  1032.5 15.8 slice-start.1
  1048.4 14.9 copy-start.38
  1048.4 14.9 copy-start.40
  1069.3 7.2 copy-start.15
  1162.7 6.0 copy-start.36
  1168.8 5.8 copy-start.16
  1168.8 5.8 copy-start.21
  1174.6 3.6 copy-start.12
  1174.6 3.6 copy-start.27
  1178.2 7.5 copy-start.28
  1319.2 3.7 copy-start.29
  1322.9 7.1 copy-start.3
  1322.9 7.1 copy-start.17
  1322.9 7.1 copy-start.35
  1323.0 7.1 copy-start.44
  1330.1 4.1 copy-start.54
  1681.2 9.3 copy-start.26
  1681.2 14.0 slice-start.2
  1681.2 14.0 slice-start.3
  1690.5 3.0 copy-start.25
  1690.5 4.7 slice-start.4
  1695.2 4.3 copy-start.24
  1699.5 3.0 copy-start.23
  1702.5 3.0 copy-start.22
  (8 other events, 9.3 us)
Sparse Core Ops, SparseCore 0:
  139.8 123.9 all-gather.6
  265.7 119.6 all-gather.4
  723.4 274.5 reduce-scatter.4
  1001.3 274.5 reduce-scatter.2
  1281.4 399.7 all-reduce.7
